TPU v7x, 32 devices: a whole 2x2x4 slice. The times are simulated.
32 devices in a mesh: sub: 32 (over z, y, x, core).
Axes of the slice: x: 2, y: 2, z: 4, core: 2. Of those that a mesh axis runs over, the one named last changes fastest.
Arguments:
- right_side: float32 [128, 128, 512], P('sub'), may hold values from -8 to 8
- sigma: float32 [128, 128, 512], P('sub'), may hold values from 0.25 to 2
- wind: float32 [128, 128, 512], P('sub'), may hold values from -0.8 to 0.8
- local_inverse: float32 [32, 512, 512], P('sub'), may hold values from -1 to 2, as said below
- basis_y: float32 [128, 32], replicated, may hold values from -0.5 to 0.5
- basis_z: float32 [512, 64], replicated, may hold values from -0.25 to 0.25
- gamma: float32 [5, 32, 64], replicated, may hold values from 0.3 to 3
Outputs:
- solution_field: float32 [128, 128, 512], P('sub')
- residual: float32 [128, 128, 512], P('sub')
Inputs may be any that keep to these rules, and one draw needn't show every extreme that they name: `local_inverse`: each block is the identity plus a perturbation whose entries lie within 2/sqrt(512) of zero; each row of the perturbation has norm about one half.
All inputs are finite; a program needn't handle non-finite values.
Results may differ from a plain program's by a relative error of at most 0.00022.
Values sent between devices are 32-bit elements; how exact they have to be, the bound alone decides.
A program may use at most 64 MiB of HBM per device.

v0:
```python
import jax
import jax.numpy as jnp
from jax import lax
from jax.sharding import PartitionSpec as P

HIGH = lax.Precision.HIGHEST


def extended(cells, sides, width):
    for axis, dim in sides:
        count = lax.axis_size(axis)
        ends = count - 1
        head = lax.slice_in_dim(cells, 0, width, axis=dim)
        tail = lax.slice_in_dim(cells, cells.shape[dim] - width, cells.shape[dim], axis=dim)
        cells = jnp.concatenate(
            [
                lax.ppermute(tail, axis, [(i, (i + 1) % count) for i in range(ends)]),
                cells,
                lax.ppermute(head, axis, [((i + 1) % count, i) for i in range(ends)]),
            ],
            axis=dim,
        )
    return cells


def swapped(block, axis, apart):
    count = lax.axis_size(axis)
    route = []
    for low in range(count):
        high = low | 1 << apart
        if high != low and high < count:
            route += [(low, high), (high, low)]
    return lax.ppermute(block, axis, route)


def apply_operator(field, sigma, wind):
    padded_x = extended(field, (("sub", 0),), 1)
    upper = padded_x[2:]
    lower = padded_x[:-2]
    padded_y = jnp.pad(field, ((0, 0), (1, 1), (0, 0)))
    padded_z = jnp.pad(field, ((0, 0), (0, 0), (1, 1)))
    beside = (
        upper
        + lower
        + padded_y[:, 2:]
        + padded_y[:, :-2]
        + padded_z[:, :, 2:]
        + padded_z[:, :, :-2]
    )
    return (6.0 + sigma) * field - beside + wind * (upper - lower)


def precondition(field, local_inverse, basis_y, basis_z, gamma):
    layers, rows, depth = field.shape
    local = jnp.dot(field.reshape(layers * rows, depth), local_inverse[0], precision=HIGH).reshape(
        layers, rows, depth
    )
    summed = jnp.sum(field, axis=0)
    proj = jnp.dot(basis_y.T, jnp.dot(summed, basis_z, precision=HIGH), precision=HIGH)
    levels = lax.axis_size("sub").bit_length() - 1
    coarse = jnp.zeros_like(proj)
    for level in range(levels):
        partial_sum = proj
        for which in range(level + 1):
            partial_sum = partial_sum + swapped(partial_sum, "sub", which)
        coarse = coarse + gamma[level] * partial_sum / jnp.sqrt(
            jnp.float32(layers * 2 ** (level + 1))
        )
    spread = jnp.dot(basis_y, jnp.dot(coarse, basis_z.T, precision=HIGH), precision=HIGH)
    return local + spread[None]


def orthogonal_step(image, vectors):
    products = [jnp.sum(vector * image) for vector in vectors]
    sums = lax.psum(jnp.stack(products + [jnp.sum(image * image)]), "sub")
    squares = sums[len(vectors)]
    for index in range(len(vectors)):
        image = image - sums[index] * vectors[index]
        squares = squares - sums[index] * sums[index]
    length = jnp.sqrt(squares)
    return (sums, image, length)


def on_device(right_side, sigma, wind, local_inverse, basis_y, basis_z, gamma):
    beta = jnp.sqrt(lax.psum(jnp.sum(right_side * right_side), "sub"))
    first = right_side / beta
    z_one = precondition(first, local_inverse, basis_y, basis_z, gamma)
    image = apply_operator(z_one, sigma, wind)
    sums, image, h21 = orthogonal_step(image, [first])
    h11 = sums[0]
    second = image / h21
    z_two = precondition(second, local_inverse, basis_y, basis_z, gamma)
    image = apply_operator(z_two, sigma, wind)
    sums, image, h32 = orthogonal_step(image, [first, second])
    h12 = sums[0]
    h22 = sums[1]
    m11 = h11 * h11 + h21 * h21
    m12 = h11 * h12 + h21 * h22
    m22 = h12 * h12 + h22 * h22 + h32 * h32
    q_one = h11 * beta
    q_two = h12 * beta
    determ = m11 * m22 - m12 * m12
    y_one = (m22 * q_one - m12 * q_two) / determ
    y_two = (m11 * q_two - m12 * q_one) / determ
    solution_field = y_one * z_one + y_two * z_two
    residual = right_side - apply_operator(solution_field, sigma, wind)
    return (solution_field, residual)


def solution(mesh):
    placed = (
        P("sub", None, None),
        P("sub", None, None),
        P("sub", None, None),
        P("sub", None, None),
        P(),
        P(),
        P(),
    )
    return jax.shard_map(
        on_device,
        mesh=mesh,
        in_specs=placed,
        out_specs=(P("sub", None, None), P("sub", None, None)),
        check_vma=False,
    )
```

profile of v0, /device:TPU:8, one launch (start us, length us, event | category | flops | bytes accessed | tf_op | source)
XLA Modules:
  0.0 225.6 jit_solution(12309424426258021769)
XLA Ops:
  0.7 2.2 multiply_reduce_fusion.5
  2.9 40.6 %psum.21 = f32[]{:T(128)} all-reduce(f32[]{:T(128)} %multiply_reduce_fusion.5), channel_id=1, replica_groups=mesh['sub'=32] {'sub'}, use_global_device_ids=true, to_apply=%region_1.0 | all-reduce | flops 1 | bytes 8 | tf_op jit(solution)/shard_map/psum | solution.py:85
  45.0 1.2 collective-permute-done
  46.2 2.3 %collective-permute-start.1 = (f32[32,64]{1,0:T(8,128)S(1)}, f32[32,64]{1,0:T(8,128)S(1)}, u32[]{:S(2)}, u32[]{:S(2)}) collective-permute-start(f32[32,64]{1,0:T(8,128)S(1)} %add.183), channel_id=1, source_target_pairs={{0,2},{2,0},{1,3},{3,1},{4,6},{6,4},{5,7},{7,5},{8,10},{10,8},{9,1... | collective-permute-start | bytes 24584 | tf_op jit(solution)/shard_map/ppermute | solution.py:33
  48.5 1.7 collective-permute-done.1
  50.2 2.2 collective-permute-start.2
  52.4 1.7 collective-permute-done.2
  54.6 3.2 %collective-permute-done.3 = f32[32,64]{1,0:T(8,128)S(1)} collective-permute-done((f32[32,64]{1,0:T(8,128)S(1)}, f32[32,64]{1,0:T(8,128)S(1)}, u32[]{:S(2)}, u32[]{:S(2)}) %collective-permute-start.3) | collective-permute-done | bytes 8224 | tf_op jit(solution)/shard_map/ppermute | solution.py:33
  57.8 1.3 collective-permute-start.4
  59.1 3.4 %collective-permute-done.4 = f32[32,64]{1,0:T(8,128)S(1)} collective-permute-done((f32[32,64]{1,0:T(8,128)S(1)}, f32[32,64]{1,0:T(8,128)S(1)}, u32[]{:S(2)}, u32[]{:S(2)}) %collective-permute-start.4) | collective-permute-done | bytes 8224 | tf_op jit(solution)/shard_map/ppermute | solution.py:33
  62.5 1.0 fusion.23
  63.5 0.6 convolution_bitcast_fusion.1
  64.2 1.9 convolution_add_fusion.1
  66.2 2.1 collective-permute-start.5
  68.3 2.4 %collective-permute-start.6 = (f32[1,128,512]{2,1,0:T(8,128)S(1)}, f32[1,128,512]{2,1,0:T(8,128)S(1)}, u32[]{:S(2)}, u32[]{:S(2)}) collective-permute-start(f32[1,128,512]{2,1,0:T(8,128)S(1)} %get-tuple-element.15), channel_id=1, source_target_pairs={{0,1},{1,2},{2,3},{3,4},{4,5},{5,6},{6,7},{7,8},{8,9},{9,10},{10,1... | collective-permute-start | bytes 786440 | tf_op jit(solution)/shard_map/ppermute | solution.py:17
  70.7 1.5 collective-permute-done.5
  72.1 5.6 %collective-permute-done.6 = f32[1,128,512]{2,1,0:T(8,128)S(1)} collective-permute-done((f32[1,128,512]{2,1,0:T(8,128)S(1)}, f32[1,128,512]{2,1,0:T(8,128)S(1)}, u32[]{:S(2)}, u32[]{:S(2)}) %collective-permute-start.6) | collective-permute-done | bytes 262176 | tf_op jit(solution)/shard_map/ppermute | solution.py:17
  77.8 1.5 multiply_reduce_fusion.4
  79.3 1.4 pad_maximum_fusion.6
  80.7 38.1 %psum.22 = f32[2]{0:T(128)S(1)} all-reduce(f32[2]{0:T(128)S(1)} %pad_maximum_fusion.6), channel_id=1, replica_groups=mesh['sub'=32] {'sub'}, use_global_device_ids=true, to_apply=%region_5.6 | all-reduce | flops 2 | bytes 16 | tf_op jit(solution)/shard_map/psum | solution.py:75
  121.3 1.9 fusion.84
  123.8 1.2 collective-permute-done.7
  125.0 2.3 %collective-permute-start.8 = (f32[32,64]{1,0:T(8,128)S(1)}, f32[32,64]{1,0:T(8,128)S(1)}, u32[]{:S(2)}, u32[]{:S(2)}) collective-permute-start(f32[32,64]{1,0:T(8,128)S(1)} %add.200), channel_id=1, source_target_pairs={{0,2},{2,0},{1,3},{3,1},{4,6},{6,4},{5,7},{7,5},{8,10},{10,8},{9,1... | collective-permute-start | bytes 24584 | tf_op jit(solution)/shard_map/ppermute | solution.py:33
  127.2 1.7 collective-permute-done.8
  129.0 2.0 collective-permute-start.9
  131.0 1.7 collective-permute-done.9
  132.7 1.6 collective-permute-start.10
  134.3 2.1 collective-permute-done.10
  136.4 2.4 %collective-permute-start.11 = (f32[32,64]{1,0:T(8,128)S(1)}, f32[32,64]{1,0:T(8,128)S(1)}, u32[]{:S(2)}, u32[]{:S(2)}) collective-permute-start(f32[32,64]{1,0:T(8,128)S(1)} %add.205), channel_id=1, source_target_pairs={{0,16},{16,0},{1,17},{17,1},{2,18},{18,2},{3,19},{19,3},{4,20},{20... | collective-permute-start | bytes 24584 | tf_op jit(solution)/shard_map/ppermute | solution.py:33
  138.9 2.2 collective-permute-done.11
  141.1 1.0 fusion.27
  142.1 0.6 convolution_bitcast_fusion
  142.8 3.1 %convolution_add_fusion = f32[4,128,512]{2,1,0:T(8,128)S(1)} fusion(f32[4,128,512]{2,1,0:T(8,128)} %get-tuple-element.8, f32[1,512,512]{2,1,0:T(8,128)S(1)} %copy-done, f32[128,512]{1,0:T(8,128)S(1)} %copy.10), kind=kOutput, calls=%fused_computation | convolution fusion | flops 1610874880 | bytes 3407872 | tf_op jit(solution)/shard_map/dot_general | solution.py:55
  145.9 0.7 fusion.87
  146.6 1.9 collective-permute-start.12
  148.5 2.4 %collective-permute-start.13 = (f32[1,128,512]{2,1,0:T(8,128)S(1)}, f32[1,128,512]{2,1,0:T(8,128)}, u32[]{:S(2)}, u32[]{:S(2)}) collective-permute-start(f32[1,128,512]{2,1,0:T(8,128)S(1)} %get-tuple-element.12), channel_id=1, source_target_pairs={{0,1},{1,2},{2,3},{3,4},{4,5},{5,6},{6,7},{7,8},{8,9},{9,10},{10,1... | collective-permute-start | bytes 786440 | tf_op jit(solution)/shard_map/ppermute | solution.py:17
  151.6 1.1 collective-permute-done.12
  152.7 5.9 %collective-permute-done.13 = f32[1,128,512]{2,1,0:T(8,128)} collective-permute-done((f32[1,128,512]{2,1,0:T(8,128)S(1)}, f32[1,128,512]{2,1,0:T(8,128)}, u32[]{:S(2)}, u32[]{:S(2)}) %collective-permute-start.13) | collective-permute-done | bytes 262176 | tf_op jit(solution)/shard_map/ppermute | solution.py:17
  158.6 3.5 %multiply_reduce_fusion.2 = (f32[]{:T(128)}, f32[]{:T(128)}, f32[]{:T(128)}) fusion(f32[4,128,512]{2,1,0:T(8,128)S(1)} %copy-done.1, f32[]{:T(128)S(6)} %sqrt.9, f32[4,128,512]{2,1,0:T(8,128)} %get-tuple-element.8, f32[4,128,512]{2,1,0:T(8,128)} %param.9, f32[4,128,512]{2,1,0:T(8,128)S(1)} %convolution_add_fusion, ...), kind=kLoop, calls=%fused_computation.48 | loop fusion | flops 5242877 | bytes 5767184 | tf_op jit(solution)/shard_map/reduce_sum | solution.py:74
  162.1 1.9 pad_maximum_fusion.7
  164.0 39.0 %psum.23 = f32[3]{0:T(128)S(1)} all-reduce(f32[3]{0:T(128)S(1)} %pad_maximum_fusion.7), channel_id=1, replica_groups=mesh['sub'=32] {'sub'}, use_global_device_ids=true, to_apply=%region_10.11 | all-reduce | flops 3 | bytes 24 | tf_op jit(solution)/shard_map/psum | solution.py:75
  203.0 0.6 fusion.89
  209.5 1.5 multiply_add_fusion
  211.1 3.1 %collective-permute-start.14 = (f32[1,128,512]{2,1,0:T(8,128)S(1)}, f32[1,128,512]{2,1,0:T(8,128)S(1)}, u32[]{:S(2)}, u32[]{:S(2)}) collective-permute-start(f32[1,128,512]{2,1,0:T(8,128)S(1)} %get-tuple-element.11), channel_id=1, source_target_pairs={{1,0},{2,1},{3,2},{4,3},{5,4},{6,5},{7,6},{8,7},{9,8},{10,9},{11,1... | collective-permute-start | bytes 786440 | tf_op jit(solution)/shard_map/ppermute | solution.py:19
  214.2 1.9 collective-permute-start.15
  216.1 1.9 collective-permute-done.14
  218.0 5.6 %collective-permute-done.15 = f32[1,128,512]{2,1,0:T(8,128)S(1)} collective-permute-done((f32[1,128,512]{2,1,0:T(8,128)S(1)}, f32[1,128,512]{2,1,0:T(8,128)S(1)}, u32[]{:S(2)}, u32[]{:S(2)}) %collective-permute-start.15) | collective-permute-done | bytes 262176 | tf_op jit(solution)/shard_map/ppermute | solution.py:17
  223.7 1.9 fusion.18
  (41 shorter events, 2.8 us)
Async XLA Ops:
  0.6 63.6 %copy-start = (f32[1,512,512]{2,1,0:T(8,128)S(1)}, f32[1,512,512]{2,1,0:T(8,128)}, u32[]{:S(2)}) copy-start(f32[1,512,512]{2,1,0:T(8,128)} %param.10) | copy-start | bytes 3145732
  0.6 43.6 %copy-start.1 = (f32[4,128,512]{2,1,0:T(8,128)S(1)}, f32[4,128,512]{2,1,0:T(8,128)}, u32[]{:S(2)}) copy-start(f32[4,128,512]{2,1,0:T(8,128)} %param.7) | copy-start | bytes 3145732
  0.7 43.7 %copy-start.8 = (f32[512,64]{0,1:T(8,128)S(1)}, f32[512,64]{0,1:T(8,128)}, u32[]{:S(2)}) copy-start(f32[512,64]{0,1:T(8,128)} %param.12) | copy-start | bytes 393220
  2.9 41.8 %copy-start.9 = (f32[128,32]{0,1:T(8,128)S(1)}, f32[128,32]{0,1:T(8,128)}, u32[]{:S(2)}) copy-start(f32[128,32]{0,1:T(8,128)} %param.11) | copy-start | bytes 49156
  44.9 1.2 collective-permute-start
  46.2 4.0 %collective-permute-start.1 = (f32[32,64]{1,0:T(8,128)S(1)}, f32[32,64]{1,0:T(8,128)S(1)}, u32[]{:S(2)}, u32[]{:S(2)}) collective-permute-start(f32[32,64]{1,0:T(8,128)S(1)} %add.183), channel_id=1, source_target_pairs={{0,2},{2,0},{1,3},{3,1},{4,6},{6,4},{5,7},{7,5},{8,10},{10,8},{9,1... | collective-permute-start | bytes 24584 | tf_op jit(solution)/shard_map/ppermute | solution.py:33
  50.2 3.9 %collective-permute-start.2 = (f32[32,64]{1,0:T(8,128)S(1)}, f32[32,64]{1,0:T(8,128)S(1)}, u32[]{:S(2)}, u32[]{:S(2)}) collective-permute-start(f32[32,64]{1,0:T(8,128)S(1)} %add.184), channel_id=1, source_target_pairs={{0,4},{4,0},{1,5},{5,1},{2,6},{6,2},{3,7},{7,3},{8,12},{12,8},{9,1... | collective-permute-start | bytes 24584 | tf_op jit(solution)/shard_map/ppermute | solution.py:33
  54.1 3.7 %collective-permute-start.3 = (f32[32,64]{1,0:T(8,128)S(1)}, f32[32,64]{1,0:T(8,128)S(1)}, u32[]{:S(2)}, u32[]{:S(2)}) collective-permute-start(f32[32,64]{1,0:T(8,128)S(1)} %add.186), channel_id=1, source_target_pairs={{0,8},{8,0},{1,9},{9,1},{2,10},{10,2},{3,11},{11,3},{4,12},{12,4},... | collective-permute-start | bytes 24584 | tf_op jit(solution)/shard_map/ppermute | solution.py:33
  57.8 4.6 %collective-permute-start.4 = (f32[32,64]{1,0:T(8,128)S(1)}, f32[32,64]{1,0:T(8,128)S(1)}, u32[]{:S(2)}, u32[]{:S(2)}) collective-permute-start(f32[32,64]{1,0:T(8,128)S(1)} %add.188), channel_id=1, source_target_pairs={{0,16},{16,0},{1,17},{17,1},{2,18},{18,2},{3,19},{19,3},{4,20},{20... | collective-permute-start | bytes 24584 | tf_op jit(solution)/shard_map/ppermute | solution.py:33
  64.2 13.5 %copy-start.4 = (f32[4,128,512]{2,1,0:T(8,128)S(1)}, f32[4,128,512]{2,1,0:T(8,128)}, u32[]{:S(2)}) copy-start(f32[4,128,512]{2,1,0:T(8,128)} %param.8) | copy-start | bytes 3145732
  66.1 13.2 %copy-start.6 = (f32[4,128,512]{2,1,0:T(8,128)}, f32[4,128,512]{2,1,0:T(8,128)S(1)}, u32[]{:S(2)}) copy-start(f32[4,128,512]{2,1,0:T(8,128)S(1)} %convolution_add_fusion.1) | copy-start | bytes 3145732
  66.2 11.6 %copy-start.2 = (f32[4,128,512]{2,1,0:T(8,128)S(1)}, f32[4,128,512]{2,1,0:T(8,128)}, u32[]{:S(2)}) copy-start(f32[4,128,512]{2,1,0:T(8,128)} %param.9) | copy-start | bytes 3145732
  66.2 5.9 %collective-permute-start.5 = (f32[1,128,512]{2,1,0:T(8,128)S(1)}, f32[1,128,512]{2,1,0:T(8,128)S(1)}, u32[]{:S(2)}, u32[]{:S(2)}) collective-permute-start(f32[1,128,512]{2,1,0:T(8,128)S(1)} %get-tuple-element.14), channel_id=1, source_target_pairs={{1,0},{2,1},{3,2},{4,3},{5,4},{6,5},{7,6},{8,7},{9,8},{10,9},{11,1... | collective-permute-start | bytes 786440 | tf_op jit(solution)/shard_map/ppermute | solution.py:19
  68.3 9.5 %collective-permute-start.6 = (f32[1,128,512]{2,1,0:T(8,128)S(1)}, f32[1,128,512]{2,1,0:T(8,128)S(1)}, u32[]{:S(2)}, u32[]{:S(2)}) collective-permute-start(f32[1,128,512]{2,1,0:T(8,128)S(1)} %get-tuple-element.15), channel_id=1, source_target_pairs={{0,1},{1,2},{2,3},{3,4},{4,5},{5,6},{6,7},{7,8},{8,9},{9,10},{10,1... | collective-permute-start | bytes 786440 | tf_op jit(solution)/shard_map/ppermute | solution.py:17
  123.7 1.2 collective-permute-start.7
  125.0 4.0 %collective-permute-start.8 = (f32[32,64]{1,0:T(8,128)S(1)}, f32[32,64]{1,0:T(8,128)S(1)}, u32[]{:S(2)}, u32[]{:S(2)}) collective-permute-start(f32[32,64]{1,0:T(8,128)S(1)} %add.200), channel_id=1, source_target_pairs={{0,2},{2,0},{1,3},{3,1},{4,6},{6,4},{5,7},{7,5},{8,10},{10,8},{9,1... | collective-permute-start | bytes 24584 | tf_op jit(solution)/shard_map/ppermute | solution.py:33
  129.0 3.7 %collective-permute-start.9 = (f32[32,64]{1,0:T(8,128)S(1)}, f32[32,64]{1,0:T(8,128)S(1)}, u32[]{:S(2)}, u32[]{:S(2)}) collective-permute-start(f32[32,64]{1,0:T(8,128)S(1)} %add.201), channel_id=1, source_target_pairs={{0,4},{4,0},{1,5},{5,1},{2,6},{6,2},{3,7},{7,3},{8,12},{12,8},{9,1... | collective-permute-start | bytes 24584 | tf_op jit(solution)/shard_map/ppermute | solution.py:33
  132.7 3.7 %collective-permute-start.10 = (f32[32,64]{1,0:T(8,128)S(1)}, f32[32,64]{1,0:T(8,128)S(1)}, u32[]{:S(2)}, u32[]{:S(2)}) collective-permute-start(f32[32,64]{1,0:T(8,128)S(1)} %add.203), channel_id=1, source_target_pairs={{0,8},{8,0},{1,9},{9,1},{2,10},{10,2},{3,11},{11,3},{4,12},{12,4},... | collective-permute-start | bytes 24584 | tf_op jit(solution)/shard_map/ppermute | solution.py:33
  136.4 4.6 %collective-permute-start.11 = (f32[32,64]{1,0:T(8,128)S(1)}, f32[32,64]{1,0:T(8,128)S(1)}, u32[]{:S(2)}, u32[]{:S(2)}) collective-permute-start(f32[32,64]{1,0:T(8,128)S(1)} %add.205), channel_id=1, source_target_pairs={{0,16},{16,0},{1,17},{17,1},{2,18},{18,2},{3,19},{19,3},{4,20},{20... | collective-permute-start | bytes 24584 | tf_op jit(solution)/shard_map/ppermute | solution.py:33
  146.6 6.1 %collective-permute-start.12 = (f32[1,128,512]{2,1,0:T(8,128)}, f32[1,128,512]{2,1,0:T(8,128)}, u32[]{:S(2)}, u32[]{:S(2)}) collective-permute-start(f32[1,128,512]{2,1,0:T(8,128)} %get-tuple-element.13), channel_id=1, source_target_pairs={{1,0},{2,1},{3,2},{4,3},{5,4},{6,5},{7,6},{8,7},{9,8},{10,9},{11,1... | collective-permute-start | bytes 786440 | tf_op jit(solution)/shard_map/ppermute | solution.py:19
  148.5 10.0 %collective-permute-start.13 = (f32[1,128,512]{2,1,0:T(8,128)S(1)}, f32[1,128,512]{2,1,0:T(8,128)}, u32[]{:S(2)}, u32[]{:S(2)}) collective-permute-start(f32[1,128,512]{2,1,0:T(8,128)S(1)} %get-tuple-element.12), channel_id=1, source_target_pairs={{0,1},{1,2},{2,3},{3,4},{4,5},{5,6},{6,7},{7,8},{8,9},{9,10},{10,1... | collective-permute-start | bytes 786440 | tf_op jit(solution)/shard_map/ppermute | solution.py:17
  209.5 14.2 %copy-start.5 = (f32[4,128,512]{2,1,0:T(8,128)S(1)}, f32[4,128,512]{2,1,0:T(8,128)}, u32[]{:S(2)}) copy-start(f32[4,128,512]{2,1,0:T(8,128)} %param.8) | copy-start | bytes 3145732
  211.0 14.5 %copy-start.7 = (f32[4,128,512]{2,1,0:T(8,128)}, f32[4,128,512]{2,1,0:T(8,128)S(1)}, u32[]{:S(2)}) copy-start(f32[4,128,512]{2,1,0:T(8,128)S(1)} %multiply_add_fusion) | copy-start | bytes 3145732
  211.0 12.6 %copy-start.3 = (f32[4,128,512]{2,1,0:T(8,128)S(1)}, f32[4,128,512]{2,1,0:T(8,128)}, u32[]{:S(2)}) copy-start(f32[4,128,512]{2,1,0:T(8,128)} %param.9) | copy-start | bytes 3145732
  211.1 7.0 %collective-permute-start.14 = (f32[1,128,512]{2,1,0:T(8,128)S(1)}, f32[1,128,512]{2,1,0:T(8,128)S(1)}, u32[]{:S(2)}, u32[]{:S(2)}) collective-permute-start(f32[1,128,512]{2,1,0:T(8,128)S(1)} %get-tuple-element.11), channel_id=1, source_target_pairs={{1,0},{2,1},{3,2},{4,3},{5,4},{6,5},{7,6},{8,7},{9,8},{10,9},{11,1... | collective-permute-start | bytes 786440 | tf_op jit(solution)/shard_map/ppermute | solution.py:19
  214.2 9.5 %collective-permute-start.15 = (f32[1,128,512]{2,1,0:T(8,128)S(1)}, f32[1,128,512]{2,1,0:T(8,128)S(1)}, u32[]{:S(2)}, u32[]{:S(2)}) collective-permute-start(f32[1,128,512]{2,1,0:T(8,128)S(1)} %get-tuple-element.10), channel_id=1, source_target_pairs={{0,1},{1,2},{2,3},{3,4},{4,5},{5,6},{6,7},{7,8},{8,9},{9,10},{10,1... | collective-permute-start | bytes 786440 | tf_op jit(solution)/shard_map/ppermute | solution.py:17
where the time goes:
time: 227 us; the launch traced here: 226 us
  blocking collectives  118 us (52%)
  waiting for transfers between devices  41.8 us (18%)
  starting transfers between devices  28.5 us (13%)
  other arithmetic  16 us (7%)
  between operations  10.1 us (4%)
  matrix products  9.18 us (4%)
  local copies, waits for them, and re-layouts  2.34 us (1%)
    psum x2, blocking collectives, orthogonal_step(): sums = lax.psum(jnp.stack(products + [jnp.sum(image * image)]), 'sub')  77 us
    psum x1, blocking collectives, on_device(): beta = jnp.sqrt(lax.psum(jnp.sum(right_side * right_side), 'sub'))  40.6 us
    ppermute x10, waiting for transfers between devices, swapped(): return lax.ppermute(block, axis, route)  20.1 us
    ppermute x3, waiting for transfers between devices, extended(): lax.ppermute(tail, axis, [(i, (i + 1) % count) for i in range(ends)])  17.1 us
    ppermute x10, starting transfers between devices, swapped(): return lax.ppermute(block, axis, route)  14.7 us
    ppermute x3, starting transfers between devices, extended(): lax.ppermute(head, axis, [((i + 1) % count, i) for i in range(ends)])  7.05 us
    ppermute x3, starting transfers between devices, extended(): lax.ppermute(tail, axis, [(i, (i + 1) % count) for i in range(ends)])  6.73 us
    reduce_sum x2, other arithmetic, orthogonal_step(): products = [jnp.sum(vector * image) for vector in vectors]  5.06 us
  transfers between devices with their start and end apart: 16, of which 16 were waited for; matrix products, arithmetic and copies ran while one was open for 0% of the time, Pallas kernels for 0%

commit v1 on v0

v1 whole, which is shorter than its diff:
```python
import functools

import jax
import jax.numpy as jnp
from jax import lax
from jax.experimental import pallas as pl
from jax.experimental.pallas import tpu as pltpu
from jax.sharding import PartitionSpec as P

HIGH = lax.Precision.HIGHEST
MESH = pl.DeviceIdType.MESH
PAD = 8


def split(x):
    hi = x.astype(jnp.bfloat16)
    lo = (x - hi.astype(jnp.float32)).astype(jnp.bfloat16)
    return hi, lo


def mm(a, b):
    return jnp.dot(a, b, preferred_element_type=jnp.float32)


def mt(a, b):
    return lax.dot_general(
        a, b, (((1,), (1,)), ((), ())), preferred_element_type=jnp.float32
    )


def tm(a, b):
    return lax.dot_general(
        a, b, (((0,), (0,)), ((), ())), preferred_element_type=jnp.float32
    )


def fold(x):
    part = jnp.sum(x, axis=0, keepdims=True)
    out = part[:, 0:128]
    for at in range(128, part.shape[1], 128):
        out = out + part[:, at : at + 128]
    return out


def kernel(
    n, block,
    r_hbm, sg_hbm, wd_hbm, li_hbm, by_hbm, bz_hbm, gm_hbm,
    x_hbm, res_hbm,
    r, sg, wd, lf, by, bz, gm, lh, ll, u1, u2, w1, w2, hs, hr, xo, ro,
    own, gat, tot, allb, low_s, low_r, nbr, gs, ggat, gtot, gall,
    in_sem, out_sem, sa, ra, sb, rb, se, re, sh, rh, sga, rga, sgb, rgb,
):
    layers, rows, depth = r.shape
    ky = by.shape[0]
    half = ky // 2
    kz = bz.shape[0]
    levels = gm.shape[0]
    blocks = n // block
    low_levels = block.bit_length() - 1
    me = lax.axis_index("sub")
    p = lax.rem(me, block)
    z = lax.div(me, block)
    us = (u1, u2)
    ws = (w1, w2)

    def load(i, src, dst):
        c = pltpu.make_async_copy(src, dst, in_sem.at[i])
        c.start()
        return c

    c_r = load(0, r_hbm, r)
    c_bz = load(1, bz_hbm, bz)
    c_by = load(2, by_hbm, by)
    c_l = load(3, li_hbm, lf)
    c_gm = load(4, gm_hbm, gm)
    c_sg = load(5, sg_hbm, sg)
    c_wd = load(6, wd_hbm, wd)

    barrier = pltpu.get_barrier_semaphore()
    in_block = [z * block + lax.rem(p + d, block) for d in range(1, block)]
    across = [lax.rem(z + d, blocks) * block + p for d in range(1, blocks)]
    first_cross = jnp.logical_and(p == 0, z > 0)
    last_cross = jnp.logical_and(p == block - 1, z < blocks - 1)

    def signal(target):
        pl.semaphore_signal(barrier, inc=1, device_id=(target,), device_id_type=MESH)

    for target in in_block + across:
        signal(target)

    @pl.when(first_cross)
    def _():
        signal(me - 1)

    @pl.when(last_cross)
    def _():
        signal(me + 1)

    zero_rows = jnp.zeros((PAD, depth), jnp.float32)
    for u in us:
        for l in range(1, layers + 1):
            u[l, 0:PAD, :] = zero_rows
            u[l, PAD + rows : PAD + rows + PAD, :] = zero_rows

    @pl.when(me == 0)
    def _():
        for k in range(2):
            us[k][0, PAD : PAD + rows, :] = jnp.zeros((rows, depth), jnp.float32)

    @pl.when(me == n - 1)
    def _():
        for k in range(2):
            us[k][layers + 1, PAD : PAD + rows, :] = jnp.zeros((rows, depth), jnp.float32)

    def send(src, dst, s, q, target):
        return pltpu.make_async_remote_copy(
            src_ref=src, dst_ref=dst, send_sem=s, recv_sem=q,
            device_id=(target,), device_id_type=MESH,
        )

    def project(k, field):
        summed = field[0]
        for l in range(1, layers):
            summed = summed + field[l]
        sh_, sl_ = split(summed)
        bh, bl = split(bz[...])
        part = mt(sh_, bh) + mt(sl_, bh) + mt(sh_, bl)
        full = jnp.dot(
            by[...], part, precision=HIGH, preferred_element_type=jnp.float32
        )
        packed = jnp.concatenate([full[0:half], full[half:ky]], axis=1)
        own[k] = packed
        gat[k, p] = packed

    def a_copy(k, d):
        return send(own.at[k], gat.at[k, p], sa.at[k, d], ra.at[k, p], in_block[d - 1])

    def a_arrived(k, d):
        q = lax.rem(p + d, block)
        return send(own.at[k], gat.at[k, q], sa.at[k, d], ra.at[k, q], in_block[d - 1])

    def b_copy(k, d):
        return send(tot.at[k], allb.at[k, z], sb.at[k, d], rb.at[k, z], across[d - 1])

    def b_arrived(k, d):
        q = lax.rem(z + d, blocks)
        return send(tot.at[k], allb.at[k, q], sb.at[k, d], rb.at[k, q], across[d - 1])

    def down(k):
        return send(hs.at[k, 0], hr.at[k, 1], sh.at[k, 0], rh.at[k, 1], me - 1)

    def up(k):
        return send(hs.at[k, 1], hr.at[k, 0], sh.at[k, 1], rh.at[k, 0], me + 1)

    def low_down(k):
        return send(low_s.at[k, 0], low_r.at[k, 1], se.at[k, 0], re.at[k, 1], me - block)

    def low_up(k):
        return send(low_s.at[k, 1], low_r.at[k, 0], se.at[k, 1], re.at[k, 0], me + block)

    def local(x):
        xh, xl = split(x)
        return mm(xh, lh[...]) + mm(xl, lh[...]) + mm(xh, ll[...])

    def factor(level):
        g = gm[level]
        return jnp.concatenate([g[0:half], g[half:ky]], axis=1) * (
            (layers * 2 ** (level + 1)) ** -0.5
        )

    def low_part(k, q, upper):
        out = None
        for level in range(low_levels):
            width = 2 ** (level + 1)
            start = lax.div(q, width) * width
            if width == block:
                acc = tot[k]
            else:
                acc = gat[k, start]
                for j in range(1, width):
                    acc = acc + gat[k, start + j]
            term = upper[level] * acc
            out = term if out is None else out + term
        return out

    def high_part(k, zz, upper):
        out = jnp.zeros(tot.shape[1:], jnp.float32)
        for level in range(low_levels, levels):
            width = 2 ** (level + 1) // block
            start = lax.div(zz, width) * width
            acc = allb[k, start]
            for j in range(1, width):
                acc = acc + allb[k, start + j]
            out = out + upper[level] * acc
        return out

    def boundary(k, field):
        first = local(field[0])
        hs[k, 0] = first

        @pl.when(me > 0)
        def _():
            down(k).start()

        us[k][1, PAD : PAD + rows, :] = first
        last = local(field[layers - 1])
        hs[k, 1] = last

        @pl.when(me < n - 1)
        def _():
            up(k).start()

        us[k][layers, PAD : PAD + rows, :] = last

    def middle(k, field):
        for l in range(1, layers - 1):
            us[k][l + 1, PAD : PAD + rows, :] = local(field[l])

    def exchange(k):
        fac = [factor(level) for level in range(levels)]
        for d in range(1, block):
            a_arrived(k, d).wait_recv()
        acc = gat[k, 0]
        for j in range(1, block):
            acc = acc + gat[k, j]
        tot[k] = acc
        allb[k, z] = acc
        for d in range(1, blocks):
            b_copy(k, d).start()

        @pl.when(jnp.logical_and(p == block - 1, z > 0))
        def _():
            low_s[k, 0] = low_part(k, 0, fac)
            low_down(k).start()

        @pl.when(jnp.logical_and(p == 0, z < blocks - 1))
        def _():
            low_s[k, 1] = low_part(k, block - 1, fac)
            low_up(k).start()

        nbr[1] = low_part(k, p, fac)

        @pl.when(p > 0)
        def _():
            nbr[0] = low_part(k, p - 1, fac)

        @pl.when(p < block - 1)
        def _():
            nbr[2] = low_part(k, p + 1, fac)

        @pl.when(jnp.logical_and(p == 0, z == 0))
        def _():
            nbr[0] = jnp.zeros(nbr.shape[1:], jnp.float32)

        @pl.when(jnp.logical_and(p == block - 1, z == blocks - 1))
        def _():
            nbr[2] = jnp.zeros(nbr.shape[1:], jnp.float32)

        for d in range(1, blocks):
            b_arrived(k, d).wait_recv()

        @pl.when(first_cross)
        def _():
            low_up(k).wait_recv()
            nbr[0] = low_r[k, 0]

        @pl.when(last_cross)
        def _():
            low_down(k).wait_recv()
            nbr[2] = low_r[k, 1]

        here = high_part(k, z, fac)
        before = high_part(k, lax.div(lax.rem(me + n - 1, n), block), fac)
        after = high_part(k, lax.div(lax.rem(me + 1, n), block), fac)
        three = []
        for c in (nbr[0] + before, nbr[1] + here, nbr[2] + after):
            three += [c[:, 0:kz], c[:, kz : 2 * kz]]
        stack = jnp.concatenate(three, axis=0)
        back = jnp.dot(
            stack, bz[...], precision=HIGH, preferred_element_type=jnp.float32
        )
        bh, bl = split(by[...])
        spreads = []
        for j in range(3):
            th, tl = split(back[j * ky : (j + 1) * ky])
            spreads.append(tm(bh, th) + tm(bl, th) + tm(bh, tl))
        u = us[k]
        mine = spreads[1]
        for l in range(1, layers + 1):
            u[l, PAD : PAD + rows, :] = u[l, PAD : PAD + rows, :] + mine
        u[0, PAD : PAD + rows, :] = jnp.where(me > 0, spreads[0], 0.0)
        u[layers + 1, PAD : PAD + rows, :] = jnp.where(me < n - 1, spreads[2], 0.0)

    step = 32

    def operator(k, l):
        u = us[k]
        col = lax.broadcasted_iota(jnp.int32, (step, depth), 1)
        for y in range(0, rows, step):
            a = PAD + y
            c = u[l + 1, a : a + step, :]
            hi = u[l + 2, a : a + step, :]
            lo = u[l, a : a + step, :]
            fwd = jnp.where(col == depth - 1, 0.0, pltpu.roll(c, depth - 1, 1))
            bwd = jnp.where(col == 0, 0.0, pltpu.roll(c, 1, 1))
            beside = (
                hi + lo + u[l + 1, a + 1 : a + step + 1, :]
                + u[l + 1, a - 1 : a + step - 1, :] + fwd + bwd
            )
            ws[k][l, y : y + step, :] = (
                (6.0 + sg[l, y : y + step, :]) * c - beside
                + wd[l, y : y + step, :] * (hi - lo)
            )

    def stencil(k):
        for l in range(1, layers - 1):
            operator(k, l)
        u = us[k]

        @pl.when(me > 0)
        def _():
            up(k).wait_recv()
            u[0, PAD : PAD + rows, :] = u[0, PAD : PAD + rows, :] + hr[k, 0]

        operator(k, 0)

        @pl.when(me < n - 1)
        def _():
            down(k).wait_recv()
            u[layers + 1, PAD : PAD + rows, :] = u[layers + 1, PAD : PAD + rows, :] + hr[k, 1]

        operator(k, layers - 1)

    def dots(pairs):
        out = []
        for a, b in pairs:
            acc = a[0] * b[0]
            for l in range(1, layers):
                acc = acc + a[l] * b[l]
            out.append(fold(acc))
        return out

    c_bz.wait()
    c_by.wait()
    c_r.wait()
    project(0, r)
    extra = jnp.where(first_cross, 1, 0) + jnp.where(last_cross, 1, 0)
    pl.semaphore_wait(barrier, block - 1 + blocks - 1 + extra)

    for d in range(1, block):
        a_copy(0, d).start()
    c_l.wait()
    big, small = split(lf[0])
    lh[...] = big
    ll[...] = small
    boundary(0, r)
    middle(0, r)
    c_gm.wait()
    exchange(0)
    c_sg.wait()
    c_wd.wait()
    stencil(0)

    project(1, w1)
    for d in range(1, block):
        a_copy(1, d).start()
    boundary(1, w1)
    middle(1, w1)
    early = dots([(r, r), (r, w1), (w1, w1)])
    exchange(1)
    stencil(1)

    late = dots([(r, w2), (w1, w2), (w2, w2)])
    blank = jnp.zeros((2, 128), jnp.float32)
    sums = jnp.concatenate(early + late + [blank], axis=0)
    gs[...] = sums
    ggat[p] = sums

    def ga_copy(d):
        return send(gs, ggat.at[p], sga.at[d], rga.at[p], in_block[d - 1])

    def ga_arrived(d):
        q = lax.rem(p + d, block)
        return send(gs, ggat.at[q], sga.at[d], rga.at[q], in_block[d - 1])

    def gb_copy(d):
        return send(gtot, gall.at[z], sgb.at[d], rgb.at[z], across[d - 1])

    def gb_arrived(d):
        q = lax.rem(z + d, blocks)
        return send(gtot, gall.at[q], sgb.at[d], rgb.at[q], across[d - 1])

    for d in range(1, block):
        ga_copy(d).start()
    for d in range(1, block):
        ga_arrived(d).wait_recv()
    acc = ggat[0]
    for j in range(1, block):
        acc = acc + ggat[j]
    gtot[...] = acc
    gall[z] = acc
    for d in range(1, blocks):
        gb_copy(d).start()
    for d in range(1, blocks):
        gb_arrived(d).wait_recv()
    acc = gall[0]
    for j in range(1, blocks):
        acc = acc + gall[j]
    full = jnp.sum(acc, axis=1, keepdims=True)
    g01, g11 = full[1:2], full[2:3]
    g02, g12, g22 = full[3:4], full[4:5], full[5:6]
    ratio = g12 / g11
    c2 = (g02 - ratio * g01) / (g22 - ratio * g12)
    c1 = g01 / g11 - ratio * c2
    outs = []
    for l in range(layers):
        for y in range(0, rows, step):
            a = PAD + y
            xo[l, y : y + step, :] = (
                c1 * u1[l + 1, a : a + step, :] + c2 * u2[l + 1, a : a + step, :]
            )
            ro[l, y : y + step, :] = (
                r[l, y : y + step, :]
                - c1 * w1[l, y : y + step, :] - c2 * w2[l, y : y + step, :]
            )
        cx = pltpu.make_async_copy(xo.at[l], x_hbm.at[l], out_sem.at[0, l])
        cr = pltpu.make_async_copy(ro.at[l], res_hbm.at[l], out_sem.at[1, l])
        cx.start()
        cr.start()
        outs += [cx, cr]

    for k in range(2):
        for d in range(1, block):
            a_copy(k, d).wait_send()
        for d in range(1, blocks):
            b_copy(k, d).wait_send()

        @pl.when(jnp.logical_and(p == block - 1, z > 0))
        def _():
            low_down(k).wait_send()

        @pl.when(jnp.logical_and(p == 0, z < blocks - 1))
        def _():
            low_up(k).wait_send()

        @pl.when(me > 0)
        def _():
            down(k).wait_send()

        @pl.when(me < n - 1)
        def _():
            up(k).wait_send()

    for d in range(1, block):
        ga_copy(d).wait_send()
    for d in range(1, blocks):
        gb_copy(d).wait_send()
    for c in outs:
        c.wait()


def on_device(right_side, sigma, wind, local_inverse, basis_y, basis_z, gamma):
    n = lax.axis_size("sub")
    block = min(8, n)
    blocks = n // block
    layers, rows, depth = right_side.shape
    ky = basis_y.shape[1]
    kz = basis_z.shape[1]
    levels = gamma.shape[0]
    f32 = jnp.float32
    packed = (ky // 2, 2 * kz)
    cube = pltpu.VMEM((layers, rows, depth), f32)
    padded = pltpu.VMEM((layers + 2, rows + 2 * PAD, depth), f32)
    dma = pltpu.SemaphoreType.DMA
    scratch = [
        cube, cube, cube,
        pltpu.VMEM((1, depth, depth), f32),
        pltpu.VMEM((ky, rows), f32),
        pltpu.VMEM((kz, depth), f32),
        pltpu.VMEM(gamma.shape, f32),
        pltpu.VMEM((depth, depth), jnp.bfloat16),
        pltpu.VMEM((depth, depth), jnp.bfloat16),
        padded, padded, cube, cube,
        pltpu.VMEM((2, 2, rows, depth), f32),
        pltpu.VMEM((2, 2, rows, depth), f32),
        cube, cube,
        pltpu.VMEM((2,) + packed, f32),
        pltpu.VMEM((2, block) + packed, f32),
        pltpu.VMEM((2,) + packed, f32),
        pltpu.VMEM((2, blocks) + packed, f32),
        pltpu.VMEM((2, 2) + packed, f32),
        pltpu.VMEM((2, 2) + packed, f32),
        pltpu.VMEM((3,) + packed, f32),
        pltpu.VMEM((8, 128), f32),
        pltpu.VMEM((block, 8, 128), f32),
        pltpu.VMEM((8, 128), f32),
        pltpu.VMEM((blocks, 8, 128), f32),
        dma((7,)), dma((2, layers)),
        dma((2, block)), dma((2, block)),
        dma((2, blocks)), dma((2, blocks)),
        dma((2, 2)), dma((2, 2)),
        dma((2, 2)), dma((2, 2)),
        dma((block,)), dma((block,)),
        dma((blocks,)), dma((blocks,)),
    ]
    anywhere = pl.BlockSpec(memory_space=pl.ANY)
    out = jax.ShapeDtypeStruct(right_side.shape, f32)
    return pl.pallas_call(
        functools.partial(kernel, n, block),
        out_shape=(out, out),
        in_specs=[anywhere] * 7,
        out_specs=(anywhere, anywhere),
        scratch_shapes=scratch,
        compiler_params=pltpu.CompilerParams(
            collective_id=0, has_side_effects=True, vmem_limit_bytes=56 * 2**20,
        ),
        name="gmres",
    )(right_side, sigma, wind, local_inverse, basis_y.T, basis_z.T, gamma)


def solution(mesh):
    placed = (
        P("sub", None, None),
        P("sub", None, None),
        P("sub", None, None),
        P("sub", None, None),
        P(),
        P(),
        P(),
    )
    return jax.shard_map(
        on_device,
        mesh=mesh,
        in_specs=placed,
        out_specs=(P("sub", None, None), P("sub", None, None)),
        check_vma=False,
    )
```

time: 227 us -> 38.7 us (0.17)
  the two profiles are of different devices: /device:TPU:8 before, /device:TPU:0 now
where the time goes in v1:
time: 38.7 us; the launch traced here: 38.5 us
  Pallas kernels  34.6 us (89%)
  local copies, waits for them, and re-layouts  3.32 us (9%)
  between operations  0.65 us (2%)
    pallas_call x1, Pallas kernels, on_device(): pl.pallas_call(functools.partial(kernel, n, block), out_shape=(out, out),...  34.6 us
    unnamed x4, local copies, waits for them, and re-layouts  3.32 us

profile of v1, /device:TPU:0, one launch (start us, length us, event | category | flops | bytes accessed | tf_op | source)
XLA Modules:
  0.0 38.5 jit_solution(7772745739751972301)
XLA Ops:
  0.6 34.6 %gmres.1 = (f32[4,128,512]{2,1,0:T(8,128)}, f32[4,128,512]{2,1,0:T(8,128)}) custom-call(f32[4,128,512]{2,1,0:T(8,128)} %r_hbm.1, f32[4,128,512]{2,1,0:T(8,128)} %sg_hbm.1, f32[4,128,512]{2,1,0:T(8,128)} %wd_hbm.1, f32[1,512,512]{2,1,0:T(8,128)} %li_hbm.1, f32[32,128]{1,0:T(8,128)} %bitcast.3, f32[64,512]{1,0:T(8,128)} %bitcast.2, f32[5,32,64]{2,1,0:T(8,128)} %gm_hbm.1), custom_call_target="tpu_custom_call" | custom-call | tf_op jit(solution)/shard_map/gmres/pallas_call | solution.py:508
  35.2 0.0 copy-start
  35.2 2.4 %copy.11 = f32[4,128,512]{2,1,0:T(8,128)} copy(f32[4,128,512]{2,1,0:T(8,128)} %get-tuple-element.4) | data formatting | bytes 2097152
  37.6 0.0 copy-done
  37.6 1.0 %copy.12 = f32[4,128,512]{2,1,0:T(8,128)} copy(f32[4,128,512]{2,1,0:T(8,128)S(1)} %copy-done) | data formatting | bytes 2097152
Async XLA Ops:
  35.2 2.4 %copy-start = (f32[4,128,512]{2,1,0:T(8,128)S(1)}, f32[4,128,512]{2,1,0:T(8,128)}, u32[]{:S(2)}) copy-start(f32[4,128,512]{2,1,0:T(8,128)} %get-tuple-element.5) | copy-start | bytes 3145732

commit v2 on v1

--- a/solution.py
+++ b/solution.py
@@ -45,10 +45,10 @@
 def kernel(
     n, block,
     r_hbm, sg_hbm, wd_hbm, li_hbm, by_hbm, bz_hbm, gm_hbm,
-    x_hbm, res_hbm,
-    r, sg, wd, lf, by, bz, gm, lh, ll, u1, u2, w1, w2, hs, hr, xo, ro,
-    own, gat, tot, allb, low_s, low_r, nbr, gs, ggat, gtot, gall,
-    in_sem, out_sem, sa, ra, sb, rb, se, re, sh, rh, sga, rga, sgb, rgb,
+    r, u1, u2, w1, w2, coef,
+    sg, wd, lf, by, bz, gm, lh, ll, hs, hr,
+    own, gat, tot, allb, low_s, low_r, nbr, gs, ggat,
+    in_sem, sa, ra, sb, rb, se, re, sh, rh, sga, rga,
 ):
     layers, rows, depth = r.shape
     ky = by.shape[0]
@@ -194,23 +194,22 @@
             out = out + upper[level] * acc
         return out
 
-    def boundary(k, field):
+    def edges(k, field):
         first = local(field[0])
         hs[k, 0] = first
-
-        @pl.when(me > 0)
-        def _():
-            down(k).start()
-
         us[k][1, PAD : PAD + rows, :] = first
         last = local(field[layers - 1])
         hs[k, 1] = last
+        us[k][layers, PAD : PAD + rows, :] = last
+
+    def send_edges(k):
+        @pl.when(me > 0)
+        def _():
+            down(k).start()
 
         @pl.when(me < n - 1)
         def _():
             up(k).start()
-
-        us[k][layers, PAD : PAD + rows, :] = last
 
     def middle(k, field):
         for l in range(1, layers - 1):
@@ -344,16 +343,16 @@
     c_by.wait()
     c_r.wait()
     project(0, r)
-    extra = jnp.where(first_cross, 1, 0) + jnp.where(last_cross, 1, 0)
-    pl.semaphore_wait(barrier, block - 1 + blocks - 1 + extra)
-
-    for d in range(1, block):
-        a_copy(0, d).start()
     c_l.wait()
     big, small = split(lf[0])
     lh[...] = big
     ll[...] = small
-    boundary(0, r)
+    edges(0, r)
+    extra = jnp.where(first_cross, 1, 0) + jnp.where(last_cross, 1, 0)
+    pl.semaphore_wait(barrier, block - 1 + blocks - 1 + extra)
+    for d in range(1, block):
+        a_copy(0, d).start()
+    send_edges(0)
     middle(0, r)
     c_gm.wait()
     exchange(0)
@@ -364,7 +363,8 @@
     project(1, w1)
     for d in range(1, block):
         a_copy(1, d).start()
-    boundary(1, w1)
+    edges(1, w1)
+    send_edges(1)
     middle(1, w1)
     early = dots([(r, r), (r, w1), (w1, w1)])
     exchange(1)
@@ -372,46 +372,63 @@
 
     late = dots([(r, w2), (w1, w2), (w2, w2)])
     blank = jnp.zeros((2, 128), jnp.float32)
-    sums = jnp.concatenate(early + late + [blank], axis=0)
-    gs[...] = sums
-    ggat[p] = sums
-
-    def ga_copy(d):
-        return send(gs, ggat.at[p], sga.at[d], rga.at[p], in_block[d - 1])
-
-    def ga_arrived(d):
-        q = lax.rem(p + d, block)
-        return send(gs, ggat.at[q], sga.at[d], rga.at[q], in_block[d - 1])
-
-    def gb_copy(d):
-        return send(gtot, gall.at[z], sgb.at[d], rgb.at[z], across[d - 1])
-
-    def gb_arrived(d):
-        q = lax.rem(z + d, blocks)
-        return send(gtot, gall.at[q], sgb.at[d], rgb.at[q], across[d - 1])
-
-    for d in range(1, block):
-        ga_copy(d).start()
-    for d in range(1, block):
-        ga_arrived(d).wait_recv()
-    acc = ggat[0]
-    for j in range(1, block):
-        acc = acc + ggat[j]
-    gtot[...] = acc
-    gall[z] = acc
-    for d in range(1, blocks):
-        gb_copy(d).start()
-    for d in range(1, blocks):
-        gb_arrived(d).wait_recv()
-    acc = gall[0]
-    for j in range(1, blocks):
-        acc = acc + gall[j]
-    full = jnp.sum(acc, axis=1, keepdims=True)
-    g01, g11 = full[1:2], full[2:3]
-    g02, g12, g22 = full[3:4], full[4:5], full[5:6]
+    sums = jnp.sum(jnp.concatenate(early + late + [blank], axis=0), axis=1, keepdims=True)
+    row = lax.broadcasted_iota(jnp.int32, (8, 128), 0)
+    lane = lax.broadcasted_iota(jnp.int32, (8, 128), 1)
+    flat = jnp.sum(jnp.where(row == lane, sums, 0.0), axis=0, keepdims=True)
+    gs[...] = flat
+    ggat[me] = flat
+
+    def g_copy(d):
+        return send(gs, ggat.at[me], sga.at[d], rga.at[me], lax.rem(me + d, n))
+
+    def g_arrived(d):
+        q = lax.rem(me + d, n)
+        return send(gs, ggat.at[q], sga.at[d], rga.at[q], q)
+
+    for d in range(1, n):
+        g_copy(d).start()
+    for d in range(1, n):
+        g_arrived(d).wait_recv()
+    total = jnp.sum(ggat[...], axis=0)
+    g01, g11, g02, g12, g22 = (total[:, j : j + 1] for j in range(1, 6))
     ratio = g12 / g11
     c2 = (g02 - ratio * g01) / (g22 - ratio * g12)
     c1 = g01 / g11 - ratio * c2
+    coef[0:1, :] = jnp.broadcast_to(c1, (1, 128))
+    coef[1:2, :] = jnp.broadcast_to(c2, (1, 128))
+
+    for k in range(2):
+        for d in range(1, block):
+            a_copy(k, d).wait_send()
+        for d in range(1, blocks):
+            b_copy(k, d).wait_send()
+
+        @pl.when(jnp.logical_and(p == block - 1, z > 0))
+        def _():
+            low_down(k).wait_send()
+
+        @pl.when(jnp.logical_and(p == 0, z < blocks - 1))
+        def _():
+            low_up(k).wait_send()
+
+        @pl.when(me > 0)
+        def _():
+            down(k).wait_send()
+
+        @pl.when(me < n - 1)
+        def _():
+            up(k).wait_send()
+
+    for d in range(1, n):
+        g_copy(d).wait_send()
+
+
+def finish(r, u1, u2, w1, w2, coef, x_hbm, res_hbm, xo, ro, out_sem):
+    layers, rows, depth = r.shape
+    step = 32
+    c1 = coef[0:1, 0:1]
+    c2 = coef[1:2, 0:1]
     outs = []
     for l in range(layers):
         for y in range(0, rows, step):
@@ -419,42 +436,18 @@
             xo[l, y : y + step, :] = (
                 c1 * u1[l + 1, a : a + step, :] + c2 * u2[l + 1, a : a + step, :]
             )
+        c = pltpu.make_async_copy(xo.at[l], x_hbm.at[l], out_sem.at[0, l])
+        c.start()
+        outs.append(c)
+    for l in range(layers):
+        for y in range(0, rows, step):
             ro[l, y : y + step, :] = (
                 r[l, y : y + step, :]
                 - c1 * w1[l, y : y + step, :] - c2 * w2[l, y : y + step, :]
             )
-        cx = pltpu.make_async_copy(xo.at[l], x_hbm.at[l], out_sem.at[0, l])
-        cr = pltpu.make_async_copy(ro.at[l], res_hbm.at[l], out_sem.at[1, l])
-        cx.start()
-        cr.start()
-        outs += [cx, cr]
-
-    for k in range(2):
-        for d in range(1, block):
-            a_copy(k, d).wait_send()
-        for d in range(1, blocks):
-            b_copy(k, d).wait_send()
-
-        @pl.when(jnp.logical_and(p == block - 1, z > 0))
-        def _():
-            low_down(k).wait_send()
-
-        @pl.when(jnp.logical_and(p == 0, z < blocks - 1))
-        def _():
-            low_up(k).wait_send()
-
-        @pl.when(me > 0)
-        def _():
-            down(k).wait_send()
-
-        @pl.when(me < n - 1)
-        def _():
-            up(k).wait_send()
-
-    for d in range(1, block):
-        ga_copy(d).wait_send()
-    for d in range(1, blocks):
-        gb_copy(d).wait_send()
+        c = pltpu.make_async_copy(ro.at[l], res_hbm.at[l], out_sem.at[1, l])
+        c.start()
+        outs.append(c)
     for c in outs:
         c.wait()
 
@@ -473,17 +466,15 @@
     padded = pltpu.VMEM((layers + 2, rows + 2 * PAD, depth), f32)
     dma = pltpu.SemaphoreType.DMA
     scratch = [
-        cube, cube, cube,
+        cube, cube,
         pltpu.VMEM((1, depth, depth), f32),
         pltpu.VMEM((ky, rows), f32),
         pltpu.VMEM((kz, depth), f32),
         pltpu.VMEM(gamma.shape, f32),
         pltpu.VMEM((depth, depth), jnp.bfloat16),
         pltpu.VMEM((depth, depth), jnp.bfloat16),
-        padded, padded, cube, cube,
         pltpu.VMEM((2, 2, rows, depth), f32),
         pltpu.VMEM((2, 2, rows, depth), f32),
-        cube, cube,
         pltpu.VMEM((2,) + packed, f32),
         pltpu.VMEM((2, block) + packed, f32),
         pltpu.VMEM((2,) + packed, f32),
@@ -491,31 +482,38 @@
         pltpu.VMEM((2, 2) + packed, f32),
         pltpu.VMEM((2, 2) + packed, f32),
         pltpu.VMEM((3,) + packed, f32),
-        pltpu.VMEM((8, 128), f32),
-        pltpu.VMEM((block, 8, 128), f32),
-        pltpu.VMEM((8, 128), f32),
-        pltpu.VMEM((blocks, 8, 128), f32),
-        dma((7,)), dma((2, layers)),
+        pltpu.VMEM((1, 128), f32),
+        pltpu.VMEM((n, 1, 128), f32),
+        dma((7,)),
         dma((2, block)), dma((2, block)),
         dma((2, blocks)), dma((2, blocks)),
         dma((2, 2)), dma((2, 2)),
         dma((2, 2)), dma((2, 2)),
-        dma((block,)), dma((block,)),
-        dma((blocks,)), dma((blocks,)),
+        dma((n,)), dma((n,)),
     ]
-    anywhere = pl.BlockSpec(memory_space=pl.ANY)
+    hbm = pl.BlockSpec(memory_space=pltpu.HBM)
+    vmem = pl.BlockSpec(memory_space=pltpu.VMEM)
     out = jax.ShapeDtypeStruct(right_side.shape, f32)
-    return pl.pallas_call(
+    pieces = pl.pallas_call(
         functools.partial(kernel, n, block),
-        out_shape=(out, out),
-        in_specs=[anywhere] * 7,
-        out_specs=(anywhere, anywhere),
+        out_shape=(cube, padded, padded, cube, cube, pltpu.VMEM((8, 128), f32)),
+        in_specs=[hbm] * 7,
+        out_specs=(vmem,) * 6,
         scratch_shapes=scratch,
         compiler_params=pltpu.CompilerParams(
-            collective_id=0, has_side_effects=True, vmem_limit_bytes=56 * 2**20,
+            collective_id=0, has_side_effects=True, vmem_limit_bytes=50 * 2**20,
         ),
         name="gmres",
     )(right_side, sigma, wind, local_inverse, basis_y.T, basis_z.T, gamma)
+    return pl.pallas_call(
+        finish,
+        out_shape=(out, out),
+        in_specs=[vmem] * 6,
+        out_specs=(hbm, hbm),
+        scratch_shapes=[cube, cube, dma((2, layers))],
+        compiler_params=pltpu.CompilerParams(vmem_limit_bytes=24 * 2**20),
+        name="finish",
+    )(*pieces)
 
 
 def solution(mesh):

time: 38.7 us -> 36.4 us (0.941)
  local copies, waits for them, and re-layouts: 3.32 us -> 0 us
  Pallas kernels: 34.6 us -> 35.6 us
    unnamed x4 -> x0, local copies, waits for them, and re-layouts: 3.32 us -> none
    pallas_call x1 -> x2, Pallas kernels: 34.6 us -> 35.6 us  [the longest x1 34.2 us: on_device(): pl.pallas_call(functools.partial(kernel, n, block), out_shape=(cube, padd...]
where the time goes in v2:
time: 36.4 us; the launch traced here: 36.2 us
  Pallas kernels  35.6 us (98%)
  between operations  0.64 us (2%)
    pallas_call x1, Pallas kernels, on_device(): pl.pallas_call(functools.partial(kernel, n, block), out_shape=(cube, padd...  34.2 us
    pallas_call x1, Pallas kernels, on_device(): pl.pallas_call(finish, out_shape=(out, out), in_specs=[vmem] * 6, out_spe...  1.44 us

profile of v2, /device:TPU:0, one launch (start us, length us, event | category | flops | bytes accessed | tf_op | source)
XLA Modules:
  0.0 36.2 jit_solution(162786305909411611)
XLA Ops:
  0.6 34.2 %gmres.1 = (f32[4,128,512]{2,1,0:T(8,128)S(1)}, f32[6,144,512]{2,1,0:T(8,128)S(1)}, f32[6,144,512]{2,1,0:T(8,128)S(1)}, f32[4,128,512]{2,1,0:T(8,128)S(1)}, f32[...) custom-call(f32[4,128,512]{2,1,0:T(8,128)} %r_hbm.1, f32[4,128,512]{2,1,0:T(8,128)} %sg_hbm.1, f32[4,128,512]{2,1,0:T(8,128)} %wd_hbm.1, ...), custom_call_target="tpu_custom_call" | custom-call | tf_op jit(solution)/shard_map/gmres/pallas_call | solution.py:497
  34.8 1.4 %finish.1 = (f32[4,128,512]{2,1,0:T(8,128)}, f32[4,128,512]{2,1,0:T(8,128)}) custom-call(f32[4,128,512]{2,1,0:T(8,128)S(1)} %get-tuple-element.8.r, f32[6,144,512]{2,1,0:T(8,128)S(1)} %get-tuple-element.9.u1, f32[6,144,512]{2,1,0:T(8,128)S(1)} %get-tuple-element.10.u2, f32[4,128,512]{2,1,0:T(8,128)S(1)} %get-tuple-element.11.w1, ...), custom_call_target="tpu_custom_call" | custom-call | tf_op jit(solution)/shard_map/finish/pallas_call | solution.py:508

commit v3 on v2

--- a/solution.py
+++ b/solution.py
@@ -46,7 +46,7 @@
     n, block,
     r_hbm, sg_hbm, wd_hbm, li_hbm, by_hbm, bz_hbm, gm_hbm,
     r, u1, u2, w1, w2, coef,
-    sg, wd, lf, by, bz, gm, lh, ll, hs, hr,
+    sg, wd, lf, by, bz, gm, lh, ll, by3, bz3, hs, hr,
     own, gat, tot, allb, low_s, low_r, nbr, gs, ggat,
     in_sem, sa, ra, sb, rb, se, re, sh, rh, sga, rga,
 ):
@@ -102,16 +102,6 @@
             u[l, 0:PAD, :] = zero_rows
             u[l, PAD + rows : PAD + rows + PAD, :] = zero_rows
 
-    @pl.when(me == 0)
-    def _():
-        for k in range(2):
-            us[k][0, PAD : PAD + rows, :] = jnp.zeros((rows, depth), jnp.float32)
-
-    @pl.when(me == n - 1)
-    def _():
-        for k in range(2):
-            us[k][layers + 1, PAD : PAD + rows, :] = jnp.zeros((rows, depth), jnp.float32)
-
     def send(src, dst, s, q, target):
         return pltpu.make_async_remote_copy(
             src_ref=src, dst_ref=dst, send_sem=s, recv_sem=q,
@@ -123,11 +113,11 @@
         for l in range(1, layers):
             summed = summed + field[l]
         sh_, sl_ = split(summed)
-        bh, bl = split(bz[...])
+        bh, bl = bz3[0:kz], bz3[2 * kz : 3 * kz]
         part = mt(sh_, bh) + mt(sl_, bh) + mt(sh_, bl)
-        full = jnp.dot(
-            by[...], part, precision=HIGH, preferred_element_type=jnp.float32
-        )
+        ph, pl_ = split(part)
+        bh, bl = by3[0:ky], by3[2 * ky : 3 * ky]
+        full = mm(bh, ph) + mm(bh, pl_) + mm(bl, ph)
         packed = jnp.concatenate([full[0:half], full[half:ky]], axis=1)
         own[k] = packed
         gat[k, p] = packed
@@ -275,14 +265,15 @@
         for c in (nbr[0] + before, nbr[1] + here, nbr[2] + after):
             three += [c[:, 0:kz], c[:, kz : 2 * kz]]
         stack = jnp.concatenate(three, axis=0)
-        back = jnp.dot(
-            stack, bz[...], precision=HIGH, preferred_element_type=jnp.float32
-        )
-        bh, bl = split(by[...])
+        th, tl = split(stack)
+        back = mm(jnp.concatenate([th, tl, th], axis=1), bz3[...])
+        th, tl = split(back)
         spreads = []
         for j in range(3):
-            th, tl = split(back[j * ky : (j + 1) * ky])
-            spreads.append(tm(bh, th) + tm(bl, th) + tm(bh, tl))
+            piece = slice(j * ky, (j + 1) * ky)
+            spreads.append(
+                tm(by3[...], jnp.concatenate([th[piece], tl[piece], th[piece]], axis=0))
+            )
         u = us[k]
         mine = spreads[1]
         for l in range(1, layers + 1):
@@ -312,35 +303,43 @@
             )
 
     def stencil(k):
-        for l in range(1, layers - 1):
+        for l in range(layers):
             operator(k, l)
-        u = us[k]
+
+    def meet(k):
+        w = ws[k]
 
         @pl.when(me > 0)
         def _():
             up(k).wait_recv()
-            u[0, PAD : PAD + rows, :] = u[0, PAD : PAD + rows, :] + hr[k, 0]
-
-        operator(k, 0)
+            w[0] = w[0] - (1.0 + wd[0]) * hr[k, 0]
 
         @pl.when(me < n - 1)
         def _():
             down(k).wait_recv()
-            u[layers + 1, PAD : PAD + rows, :] = u[layers + 1, PAD : PAD + rows, :] + hr[k, 1]
-
-        operator(k, layers - 1)
-
-    def dots(pairs):
+            w[layers - 1] = w[layers - 1] + (wd[layers - 1] - 1.0) * hr[k, 1]
+
+    def dots(pairs, which):
         out = []
         for a, b in pairs:
-            acc = a[0] * b[0]
-            for l in range(1, layers):
-                acc = acc + a[l] * b[l]
+            acc = None
+            for l in which:
+                term = a[l] * b[l]
+                acc = term if acc is None else acc + term
             out.append(fold(acc))
         return out
 
+    def triple(src, dst):
+        hi, lo = split(src[...])
+        m = src.shape[0]
+        dst[0:m] = hi
+        dst[m : 2 * m] = hi
+        dst[2 * m : 3 * m] = lo
+
     c_bz.wait()
+    triple(bz, bz3)
     c_by.wait()
+    triple(by, by3)
     c_r.wait()
     project(0, r)
     c_l.wait()
@@ -352,25 +351,28 @@
     pl.semaphore_wait(barrier, block - 1 + blocks - 1 + extra)
     for d in range(1, block):
         a_copy(0, d).start()
+    middle(0, r)
     send_edges(0)
-    middle(0, r)
     c_gm.wait()
     exchange(0)
     c_sg.wait()
     c_wd.wait()
     stencil(0)
+    meet(0)
 
     project(1, w1)
     for d in range(1, block):
         a_copy(1, d).start()
     edges(1, w1)
+    middle(1, w1)
     send_edges(1)
-    middle(1, w1)
-    early = dots([(r, r), (r, w1), (w1, w1)])
+    early = dots([(r, r), (r, w1), (w1, w1)], range(layers))
     exchange(1)
     stencil(1)
-
-    late = dots([(r, w2), (w1, w2), (w2, w2)])
+    pairs = [(r, w2), (w1, w2), (w2, w2)]
+    inside = dots(pairs, range(1, layers - 1))
+    meet(1)
+    late = [i + o for i, o in zip(inside, dots(pairs, (0, layers - 1)))]
     blank = jnp.zeros((2, 128), jnp.float32)
     sums = jnp.sum(jnp.concatenate(early + late + [blank], axis=0), axis=1, keepdims=True)
     row = lax.broadcasted_iota(jnp.int32, (8, 128), 0)
@@ -473,6 +475,8 @@
         pltpu.VMEM(gamma.shape, f32),
         pltpu.VMEM((depth, depth), jnp.bfloat16),
         pltpu.VMEM((depth, depth), jnp.bfloat16),
+        pltpu.VMEM((3 * ky, rows), jnp.bfloat16),
+        pltpu.VMEM((3 * kz, depth), jnp.bfloat16),
         pltpu.VMEM((2, 2, rows, depth), f32),
         pltpu.VMEM((2, 2, rows, depth), f32),
         pltpu.VMEM((2,) + packed, f32),

time: 36.4 us -> 34.3 us (0.942)
  Pallas kernels: 35.6 us -> 33.5 us
    pallas_call x1, Pallas kernels: 34.2 us -> 32.1 us  [on_device(): pl.pallas_call(functools.partial(kernel, n, block), out_shape=(cube, padd...]
where the time goes in v3:
time: 34.3 us; the launch traced here: 34.2 us
  Pallas kernels  33.5 us (98%)
  between operations  0.64 us (2%)
    pallas_call x1, Pallas kernels, on_device(): pl.pallas_call(functools.partial(kernel, n, block), out_shape=(cube, padd...  32.1 us
    pallas_call x1, Pallas kernels, on_device(): pl.pallas_call(finish, out_shape=(out, out), in_specs=[vmem] * 6, out_spe...  1.44 us

profile of v3, /device:TPU:0, one launch (start us, length us, event | category | flops | bytes accessed | tf_op | source)
XLA Modules:
  0.0 34.2 jit_solution(15027003302601718728)
XLA Ops:
  0.6 32.1 %gmres.1 = (f32[4,128,512]{2,1,0:T(8,128)S(1)}, f32[6,144,512]{2,1,0:T(8,128)S(1)}, f32[6,144,512]{2,1,0:T(8,128)S(1)}, f32[4,128,512]{2,1,0:T(8,128)S(1)}, f32[...) custom-call(f32[4,128,512]{2,1,0:T(8,128)} %r_hbm.1, f32[4,128,512]{2,1,0:T(8,128)} %sg_hbm.1, f32[4,128,512]{2,1,0:T(8,128)} %wd_hbm.1, ...), custom_call_target="tpu_custom_call" | custom-call | tf_op jit(solution)/shard_map/gmres/pallas_call | solution.py:501
  32.7 1.4 %finish.1 = (f32[4,128,512]{2,1,0:T(8,128)}, f32[4,128,512]{2,1,0:T(8,128)}) custom-call(f32[4,128,512]{2,1,0:T(8,128)S(1)} %get-tuple-element.8.r, f32[6,144,512]{2,1,0:T(8,128)S(1)} %get-tuple-element.9.u1, f32[6,144,512]{2,1,0:T(8,128)S(1)} %get-tuple-element.10.u2, f32[4,128,512]{2,1,0:T(8,128)S(1)} %get-tuple-element.11.w1, ...), custom_call_target="tpu_custom_call" | custom-call | tf_op jit(solution)/shard_map/finish/pallas_call | solution.py:512

commit v4 on v3

--- a/solution.py
+++ b/solution.py
@@ -73,8 +73,6 @@
     c_by = load(2, by_hbm, by)
     c_l = load(3, li_hbm, lf)
     c_gm = load(4, gm_hbm, gm)
-    c_sg = load(5, sg_hbm, sg)
-    c_wd = load(6, wd_hbm, wd)
 
     barrier = pltpu.get_barrier_semaphore()
     in_block = [z * block + lax.rem(p + d, block) for d in range(1, block)]
@@ -187,19 +185,20 @@
     def edges(k, field):
         first = local(field[0])
         hs[k, 0] = first
+
+        @pl.when(me > 0)
+        def _():
+            down(k).start()
+
         us[k][1, PAD : PAD + rows, :] = first
         last = local(field[layers - 1])
         hs[k, 1] = last
+
+        @pl.when(me < n - 1)
+        def _():
+            up(k).start()
+
         us[k][layers, PAD : PAD + rows, :] = last
-
-    def send_edges(k):
-        @pl.when(me > 0)
-        def _():
-            down(k).start()
-
-        @pl.when(me < n - 1)
-        def _():
-            up(k).start()
 
     def middle(k, field):
         for l in range(1, layers - 1):
@@ -342,17 +341,18 @@
     triple(by, by3)
     c_r.wait()
     project(0, r)
+    extra = jnp.where(first_cross, 1, 0) + jnp.where(last_cross, 1, 0)
+    pl.semaphore_wait(barrier, block - 1 + blocks - 1 + extra)
+    for d in range(1, block):
+        a_copy(0, d).start()
     c_l.wait()
+    c_sg = load(5, sg_hbm, sg)
+    c_wd = load(6, wd_hbm, wd)
     big, small = split(lf[0])
     lh[...] = big
     ll[...] = small
     edges(0, r)
-    extra = jnp.where(first_cross, 1, 0) + jnp.where(last_cross, 1, 0)
-    pl.semaphore_wait(barrier, block - 1 + blocks - 1 + extra)
-    for d in range(1, block):
-        a_copy(0, d).start()
     middle(0, r)
-    send_edges(0)
     c_gm.wait()
     exchange(0)
     c_sg.wait()
@@ -365,7 +365,6 @@
         a_copy(1, d).start()
     edges(1, w1)
     middle(1, w1)
-    send_edges(1)
     early = dots([(r, r), (r, w1), (w1, w1)], range(layers))
     exchange(1)
     stencil(1)

time: 34.3 us -> 32.6 us (0.950)
  Pallas kernels: 33.5 us -> 31.8 us
    pallas_call x1, Pallas kernels: 32.1 us -> 30.4 us  [on_device(): pl.pallas_call(functools.partial(kernel, n, block), out_shape=(cube, padd...]
where the time goes in v4:
time: 32.6 us; the launch traced here: 32.4 us
  Pallas kernels  31.8 us (98%)
  between operations  0.64 us (2%)
    pallas_call x1, Pallas kernels, on_device(): pl.pallas_call(functools.partial(kernel, n, block), out_shape=(cube, padd...  30.4 us
    pallas_call x1, Pallas kernels, on_device(): pl.pallas_call(finish, out_shape=(out, out), in_specs=[vmem] * 6, out_spe...  1.44 us

profile of v4, /device:TPU:0, one launch (start us, length us, event | category | flops | bytes accessed | tf_op | source)
XLA Modules:
  0.0 32.4 jit_solution(11225971055158977164)
XLA Ops:
  0.6 30.4 %gmres.1 = (f32[4,128,512]{2,1,0:T(8,128)S(1)}, f32[6,144,512]{2,1,0:T(8,128)S(1)}, f32[6,144,512]{2,1,0:T(8,128)S(1)}, f32[4,128,512]{2,1,0:T(8,128)S(1)}, f32[...) custom-call(f32[4,128,512]{2,1,0:T(8,128)} %r_hbm.1, f32[4,128,512]{2,1,0:T(8,128)} %sg_hbm.1, f32[4,128,512]{2,1,0:T(8,128)} %wd_hbm.1, ...), custom_call_target="tpu_custom_call" | custom-call | tf_op jit(solution)/shard_map/gmres/pallas_call | solution.py:500
  31.0 1.4 %finish.1 = (f32[4,128,512]{2,1,0:T(8,128)}, f32[4,128,512]{2,1,0:T(8,128)}) custom-call(f32[4,128,512]{2,1,0:T(8,128)S(1)} %get-tuple-element.8.r, f32[6,144,512]{2,1,0:T(8,128)S(1)} %get-tuple-element.9.u1, f32[6,144,512]{2,1,0:T(8,128)S(1)} %get-tuple-element.10.u2, f32[4,128,512]{2,1,0:T(8,128)S(1)} %get-tuple-element.11.w1, ...), custom_call_target="tpu_custom_call" | custom-call | tf_op jit(solution)/shard_map/finish/pallas_call | solution.py:511
